TPU v7x, 32 devices: a whole 2x2x4 slice. The times are simulated.
32 devices in a mesh: snap: 2 (over y), row: 8 (over z, x), col: 2 (over core).
Axes of the slice: x: 2, y: 2, z: 4, core: 2. Of those that a mesh axis runs over, the one named last changes fastest.
Arguments:
- density: bfloat16 [8192, 1024], P(('snap', 'row'), 'col'), parts along dimension 0, may hold values from -0.5 to 2
- pattern: int32 [256, 32], P(('snap', 'row'), 'col'), parts along dimension 0, may hold values 0 or 1
- filter_mask: int32 [256, 32], P(('snap', 'row')), parts along dimension 0, may hold values 0 or 1
Outputs:
- purified: bfloat16 [8192, 1024], P(('snap', 'row'), 'col'), parts along dimension 0
- traces: float32 [4], P('snap'), parts along dimension 0
There are 2 independent parts, one for each index of `snap`. A program takes and returns all parts, laid end to end along the dimension named above; each array names one. Nothing has to cross between parts.
All inputs are finite; a program needn't handle non-finite values. No bound on the sum of `pattern` or of `filter_mask` on one device may be relied on, other than what follows from the above.
Results may differ from a plain program's by a relative error of at most 0.006.
Values may be sent and summed in bfloat16 or wider, within the bound.
A program may use at most 64 MiB of HBM per device.

v0:
```python
import jax
import jax.numpy as jnp
from jax import lax
from jax.sharding import PartitionSpec as P

BLK = 32


def extended_2(value, sides, width):
    for axis, dim in sides:
        size, length = (lax.axis_size(axis), value.shape[dim])
        up = [(i, (i + 1) % size) for i in range(size - 1)]
        down = [(j, i) for i, j in up]
        last = lax.slice_in_dim(value, length - width, length, axis=dim)
        leading = lax.slice_in_dim(value, 0, width, axis=dim)
        before = lax.ppermute(last, axis, up)
        after = lax.ppermute(leading, axis, down)
        value = jnp.concatenate([before, value, after], axis=dim)
    return value


def valid_slots(first_row, row_count, first_slot, slot_count, half_band, block_total):
    row_index = first_row + jnp.arange(row_count, dtype=jnp.int32)
    slot_index = first_slot + jnp.arange(slot_count, dtype=jnp.int32)
    column_index = row_index[:, None] + slot_index[None, :] - half_band
    return ((column_index >= 0) & (column_index < block_total)).astype(jnp.int32)


def expand_mask(values, keep_mask):
    block_rows = keep_mask.shape[0]
    slot_count = keep_mask.shape[1]
    blocks = values.reshape(block_rows, BLK, slot_count, BLK)
    blocks = blocks * keep_mask.astype(values.dtype)[:, None, :, None]
    return blocks.reshape(block_rows * BLK, slot_count * BLK)


def shift_slots(segment, moved):
    height = segment.shape[0]
    if moved > 0:
        return jnp.concatenate(
            [
                jnp.zeros((height, moved * BLK), segment.dtype),
                segment[:, : segment.shape[1] - moved * BLK],
            ],
            1,
        )
    if moved < 0:
        return jnp.concatenate(
            [segment[:, -moved * BLK :], jnp.zeros((height, -moved * BLK), segment.dtype)], 1
        )
    return segment


def band_part(left, extended, first_slot, column_slots, slot_count, half_band):
    block_rows = left.shape[0] // BLK
    byte_limit = 4 * 1024 * 1024
    group_rows = 1
    for candidate in (8, 4, 2):
        if (
            block_rows % candidate == 0
            and candidate * slot_count * BLK * column_slots * BLK * 2 <= byte_limit
        ):
            group_rows = candidate
            break

    def one_group(group):
        first = group * group_rows
        stacked = []
        for offset in range(slot_count):
            segment = lax.dynamic_slice_in_dim(
                extended, (first + offset) * BLK, group_rows * BLK, 0
            )
            segment = shift_slots(segment, offset - half_band)
            segment = lax.dynamic_slice_in_dim(segment, first_slot * BLK, column_slots * BLK, 1)
            stacked.append(segment.reshape(group_rows, BLK, column_slots * BLK))
        gathered = jnp.stack(stacked, 1).reshape(group_rows, slot_count * BLK, column_slots * BLK)
        left_rows = lax.dynamic_slice_in_dim(left, first * BLK, group_rows * BLK, 0).reshape(
            group_rows, BLK, slot_count * BLK
        )
        result = jnp.einsum("gak,gkn->gan", left_rows, gathered, preferred_element_type=jnp.float32)
        return result.reshape(group_rows * BLK, column_slots * BLK)

    result = lax.map(one_group, jnp.arange(block_rows // group_rows, dtype=jnp.int32))
    return result.reshape(block_rows * BLK, column_slots * BLK)


def diagonal_sum(values, chosen):
    block_rows = values.shape[0] // BLK
    slot_total = values.shape[1] // BLK
    diagonal = jnp.diagonal(values.reshape(block_rows, BLK, slot_total, BLK), axis1=1, axis2=3)
    return jnp.sum(diagonal.astype(jnp.float32) * chosen[None, :, None])


def slot_products(
    full_rows, extended, own_filter, first_slot, half_slots, slot_count, half_band, collect
):
    square = band_part(full_rows, extended, first_slot, half_slots, slot_count, half_band)
    squared = expand_mask(square, own_filter).astype(jnp.bfloat16)
    squared_rows = collect(squared)
    cube = band_part(squared_rows, extended, first_slot, half_slots, slot_count, half_band)
    purified = (3.0 * squared.astype(jnp.float32) - 2.0 * expand_mask(cube, own_filter)).astype(
        jnp.bfloat16
    )
    return (purified, squared)


def per_device(density, pattern, filter_mask):
    half_slots = density.shape[1] // BLK
    slot_count = 2 * half_slots
    block_rows = density.shape[0] // BLK
    col_id = lax.axis_index("col")
    row_id = lax.axis_index("row")
    block_total = block_rows * lax.axis_size("row")
    first_slot = col_id * half_slots
    own_valid = valid_slots(
        row_id * block_rows, block_rows, first_slot, half_slots, half_slots, block_total
    )
    kept = expand_mask(density, pattern * own_valid)
    chosen = (first_slot + jnp.arange(half_slots, dtype=jnp.int32) == half_slots).astype(
        jnp.float32
    )
    trace_kept = diagonal_sum(kept, chosen)
    total_kept = lax.psum(trace_kept, ("row", "col"))
    own_filter = lax.dynamic_slice_in_dim(filter_mask, first_slot, half_slots, 1) * own_valid
    rim_rows = extended_2(kept, (("row", 0),), half_slots * BLK)
    extended = lax.all_gather(rim_rows, "col", axis=1, tiled=True)
    full_rows = extended[half_slots * BLK : half_slots * BLK + block_rows * BLK]

    def collect_half(squared):
        return lax.all_gather(squared, "col", axis=1, tiled=True)

    purified, squared = slot_products(
        full_rows,
        extended,
        own_filter,
        first_slot,
        half_slots,
        slot_count,
        half_slots,
        collect_half,
    )
    trace_squared = diagonal_sum(squared, chosen)
    total_squared = lax.psum(trace_squared, ("row", "col"))
    order_total = block_total * BLK
    traces = jnp.stack([total_kept, total_squared]) / order_total
    return (purified, traces)


def solution(mesh):
    return jax.shard_map(
        per_device,
        mesh=mesh,
        in_specs=(P(("snap", "row"), "col"), P(("snap", "row"), "col"), P(("snap", "row"), None)),
        out_specs=(P(("snap", "row"), "col"), P("snap")),
        check_vma=False,
    )
```

profile of v0, /device:TPU:0, one launch (start us, length us, event | category | flops | bytes accessed | tf_op | source)
XLA Modules:
  0.0 517.6 jit_solution(5589783563380693730)
XLA Ops:
  8.4 2.1 mul.804
  10.6 4.9 collective-permute-start
  16.8 21.1 %collective-permute-done = bf16[512,512]{1,0:T(8,128)(2,1)S(1)} collective-permute-done((bf16[512,512]{1,0:T(8,128)(2,1)S(1)}, bf16[512,512]{1,0:T(8,128)(2,1)S(1)}, u32[]{:S(2)}, u32[]{:S(2)}) %collective-permute-start) | collective-permute-done | bytes 524320 | tf_op jit(solution)/shard_map/ppermute | solution.py:16
  40.5 4.3 copy.7
  44.8 2.4 mul.808.clone
  47.2 4.7 mul.809
  51.9 1.8 all-gather.3.cloned.1.call-done
  53.7 2.3 slice.442
  57.1 199.7 %while.26 = (s32[]{:T(128)}, f32[4,128,512]{2,1,0:T(8,128)}, s32[4]{0:T(128)S(1)}, bf16[512,1024]{1,0:T(8,128)(2,1)}, bf16[1536,1024]{1,0:T(8,128)(2,1)}, /*inde...) while((s32[]{:T(128)}, f32[4,128,512]{2,1,0:T(8,128)}, ...), condition=%wide.region_1.2_spmd, body=%wide.region_0.1_spmd.sunk | while | flops 134217904 | bytes 56200764 | solution.py:83
  60.3 1.7 constant_dynamic-slice_fusion.66
  103.3 3.0 fusion.27
  110.3 1.7 constant_dynamic-slice_fusion.66
  153.2 3.0 fusion.27
  160.2 1.7 constant_dynamic-slice_fusion.66
  203.1 3.0 fusion.27
  210.1 1.7 constant_dynamic-slice_fusion.66
  253.0 3.0 fusion.27
  256.7 2.5 fusion.4
  259.2 4.6 multiply_bitcast_fusion
  263.8 2.8 gather_fusion
  266.7 2.7 reshape_reshape.10
  269.4 7.3 %copy.8 = f32[16,32,16,32]{2,0,3,1:T(8,128)} copy(f32[16,32,16,32]{3,2,1,0:T(8,128)} %reshape_reshape.10) | data formatting | bytes 2097152 | tf_op jit(solution)/shard_map/reshape;reshape | solution.py:32
  276.6 6.8 %fusion = bf16[16,16,32,32]{1,0,3,2:T(8,128)(2,1)} fusion(f32[16,32,16,32]{2,0,3,1:T(8,128)} %copy.8, f32[16,16]{1,0:T(8,128)S(1)} %get-tuple-element.403), kind=kLoop, calls=%fused_computation.163 | loop fusion | flops 524288 | bytes 1573888 | tf_op jit(solution)/shard_map/jit(diagonal)/transpose | solution.py:90
  283.4 2.8 gather_fusion.1
  287.0 34.8 %all-reduce.62 = (f32[1]{0:T(128)}, f32[1]{0:T(128)}) all-reduce(f32[1]{0:T(128)} %bitcast.140, f32[1]{0:T(128)} %bitcast.138), channel_id=1, replica_groups=mesh['snap'=2,'row'=8,'col'=2] {'row','col'}, use_global_device_ids=true, to_apply=%region_7.8 | all-reduce | flops 2 | bytes 16 | tf_op jit(solution)/shard_map/psum | solution.py:143
  321.9 1.8 maximum_multiply_fusion
  324.8 183.3 %while.27 = (s32[]{:T(128)}, f32[4,128,512]{2,1,0:T(8,128)}, s32[4]{0:T(128)S(1)}, bf16[512,1024]{1,0:T(8,128)(2,1)}, bf16[1536,1024]{1,0:T(8,128)(2,1)S(1)}, /*...) while((s32[]{:T(128)}, f32[4,128,512]{2,1,0:T(8,128)}, ...), condition=%wide.region_3.4_spmd, body=%wide.region_2.3_spmd.sunk | while | flops 134217904 | bytes 43617860 | solution.py:83
  366.9 3.0 fusion.31
  412.7 3.0 fusion.31
  458.5 3.0 fusion.31
  504.3 3.0 fusion.31
  508.0 2.8 fusion.3
  (726 shorter events, 347.1 us)
Async XLA Ops:
  7.2 46.5 %all-gather.3.cloned.1.call-start = ((), (), s32[]{:S(2)}) async-start(), calls=%async_computation | async-start | bytes 4718592 | tf_op jit(solution)/shard_map/all_gather | solution.py:126
  10.6 27.3 %collective-permute-start = (bf16[512,512]{1,0:T(8,128)(2,1)S(1)}, bf16[512,512]{1,0:T(8,128)(2,1)S(1)}, u32[]{:S(2)}, u32[]{:S(2)}) collective-permute-start(bf16[512,512]{1,0:T(8,128)(2,1)S(1)} %mul.805), channel_id=1, source_target_pairs={{0,2},{2,4},{4,6},{6,8},{8,10},{10,12},{12,14},{1,3},{3,5},{5,7},{... | collective-permute-start | bytes 1572872 | tf_op jit(solution)/shard_map/ppermute | solution.py:16
  15.5 22.4 %collective-permute-start.1 = (bf16[512,512]{1,0:T(8,128)(2,1)S(1)}, bf16[512,512]{1,0:T(8,128)(2,1)S(1)}, u32[]{:S(2)}, u32[]{:S(2)}) collective-permute-start(bf16[512,512]{1,0:T(8,128)(2,1)S(1)} %mul.805), channel_id=1, source_target_pairs={{2,0},{4,2},{6,4},{8,6},{10,8},{12,10},{14,12},{3,1},{5,3},{7,5},{... | collective-permute-start | bytes 1572872 | tf_op jit(solution)/shard_map/ppermute | solution.py:17
  39.2 284.5 %all-gather.5.cloned.1.call-start = ((), (), s32[]{:S(2)}) async-start(), calls=%async_computation.1 | async-start | bytes 1572864 | tf_op jit(solution)/shard_map/all_gather | solution.py:130
  57.1 13.0 %copy-start = (bf16[1536,1024]{1,0:T(8,128)(2,1)S(1)}, bf16[1536,1024]{1,0:T(8,128)(2,1)}, u32[]{:S(2)}) copy-start(bf16[1536,1024]{1,0:T(8,128)(2,1)} %get-tuple-element.866) | copy-start | bytes 9437188 | tf_op jit(solution)/shard_map/while
  87.8 11.5 %copy-start.18 = (bf16[128,640]{1,0:T(8,128)(2,1)S(1)}, bf16[128,640]{1,0:T(8,128)(2,1)}, u32[]{:S(2)}) copy-start(bf16[128,640]{1,0:T(8,128)(2,1)} %get-tuple-element.664) | copy-start | bytes 491524 | tf_op jit(solution)/shard_map/while
  87.8 11.5 %copy-start.20 = (bf16[128,608]{1,0:T(8,128)(2,1)S(1)}, bf16[128,608]{1,0:T(8,128)(2,1)}, u32[]{:S(2)}) copy-start(bf16[128,608]{1,0:T(8,128)(2,1)} %get-tuple-element.663) | copy-start | bytes 466948 | tf_op jit(solution)/shard_map/while
  88.1 12.7 %copy-start.14 = (bf16[128,576]{1,0:T(8,128)(2,1)S(1)}, bf16[128,576]{1,0:T(8,128)(2,1)}, u32[]{:S(2)}) copy-start(bf16[128,576]{1,0:T(8,128)(2,1)} %get-tuple-element.668) | copy-start | bytes 442372 | tf_op jit(solution)/shard_map/while
  88.1 12.6 %copy-start.16 = (bf16[128,544]{1,0:T(8,128)(2,1)S(1)}, bf16[128,544]{1,0:T(8,128)(2,1)}, u32[]{:S(2)}) copy-start(bf16[128,544]{1,0:T(8,128)(2,1)} %get-tuple-element.667) | copy-start | bytes 417796 | tf_op jit(solution)/shard_map/while
  107.0 13.0 %copy-start = (bf16[1536,1024]{1,0:T(8,128)(2,1)S(1)}, bf16[1536,1024]{1,0:T(8,128)(2,1)}, u32[]{:S(2)}) copy-start(bf16[1536,1024]{1,0:T(8,128)(2,1)} %get-tuple-element.866) | copy-start | bytes 9437188 | tf_op jit(solution)/shard_map/while
  137.7 11.5 %copy-start.18 = (bf16[128,640]{1,0:T(8,128)(2,1)S(1)}, bf16[128,640]{1,0:T(8,128)(2,1)}, u32[]{:S(2)}) copy-start(bf16[128,640]{1,0:T(8,128)(2,1)} %get-tuple-element.664) | copy-start | bytes 491524 | tf_op jit(solution)/shard_map/while
  137.8 11.5 %copy-start.20 = (bf16[128,608]{1,0:T(8,128)(2,1)S(1)}, bf16[128,608]{1,0:T(8,128)(2,1)}, u32[]{:S(2)}) copy-start(bf16[128,608]{1,0:T(8,128)(2,1)} %get-tuple-element.663) | copy-start | bytes 466948 | tf_op jit(solution)/shard_map/while
  138.1 12.7 %copy-start.14 = (bf16[128,576]{1,0:T(8,128)(2,1)S(1)}, bf16[128,576]{1,0:T(8,128)(2,1)}, u32[]{:S(2)}) copy-start(bf16[128,576]{1,0:T(8,128)(2,1)} %get-tuple-element.668) | copy-start | bytes 442372 | tf_op jit(solution)/shard_map/while
  138.1 12.6 %copy-start.16 = (bf16[128,544]{1,0:T(8,128)(2,1)S(1)}, bf16[128,544]{1,0:T(8,128)(2,1)}, u32[]{:S(2)}) copy-start(bf16[128,544]{1,0:T(8,128)(2,1)} %get-tuple-element.667) | copy-start | bytes 417796 | tf_op jit(solution)/shard_map/while
  156.9 13.0 %copy-start = (bf16[1536,1024]{1,0:T(8,128)(2,1)S(1)}, bf16[1536,1024]{1,0:T(8,128)(2,1)}, u32[]{:S(2)}) copy-start(bf16[1536,1024]{1,0:T(8,128)(2,1)} %get-tuple-element.866) | copy-start | bytes 9437188 | tf_op jit(solution)/shard_map/while
  187.7 11.5 %copy-start.18 = (bf16[128,640]{1,0:T(8,128)(2,1)S(1)}, bf16[128,640]{1,0:T(8,128)(2,1)}, u32[]{:S(2)}) copy-start(bf16[128,640]{1,0:T(8,128)(2,1)} %get-tuple-element.664) | copy-start | bytes 491524 | tf_op jit(solution)/shard_map/while
  188.0 12.7 %copy-start.14 = (bf16[128,576]{1,0:T(8,128)(2,1)S(1)}, bf16[128,576]{1,0:T(8,128)(2,1)}, u32[]{:S(2)}) copy-start(bf16[128,576]{1,0:T(8,128)(2,1)} %get-tuple-element.668) | copy-start | bytes 442372 | tf_op jit(solution)/shard_map/while
  188.0 12.6 %copy-start.16 = (bf16[128,544]{1,0:T(8,128)(2,1)S(1)}, bf16[128,544]{1,0:T(8,128)(2,1)}, u32[]{:S(2)}) copy-start(bf16[128,544]{1,0:T(8,128)(2,1)} %get-tuple-element.667) | copy-start | bytes 417796 | tf_op jit(solution)/shard_map/while
  206.8 13.0 %copy-start = (bf16[1536,1024]{1,0:T(8,128)(2,1)S(1)}, bf16[1536,1024]{1,0:T(8,128)(2,1)}, u32[]{:S(2)}) copy-start(bf16[1536,1024]{1,0:T(8,128)(2,1)} %get-tuple-element.866) | copy-start | bytes 9437188 | tf_op jit(solution)/shard_map/while
  237.6 11.5 %copy-start.18 = (bf16[128,640]{1,0:T(8,128)(2,1)S(1)}, bf16[128,640]{1,0:T(8,128)(2,1)}, u32[]{:S(2)}) copy-start(bf16[128,640]{1,0:T(8,128)(2,1)} %get-tuple-element.664) | copy-start | bytes 491524 | tf_op jit(solution)/shard_map/while
  237.6 11.5 %copy-start.20 = (bf16[128,608]{1,0:T(8,128)(2,1)S(1)}, bf16[128,608]{1,0:T(8,128)(2,1)}, u32[]{:S(2)}) copy-start(bf16[128,608]{1,0:T(8,128)(2,1)} %get-tuple-element.663) | copy-start | bytes 466948 | tf_op jit(solution)/shard_map/while
  237.9 12.7 %copy-start.14 = (bf16[128,576]{1,0:T(8,128)(2,1)S(1)}, bf16[128,576]{1,0:T(8,128)(2,1)}, u32[]{:S(2)}) copy-start(bf16[128,576]{1,0:T(8,128)(2,1)} %get-tuple-element.668) | copy-start | bytes 442372 | tf_op jit(solution)/shard_map/while
  237.9 12.6 %copy-start.16 = (bf16[128,544]{1,0:T(8,128)(2,1)S(1)}, bf16[128,544]{1,0:T(8,128)(2,1)}, u32[]{:S(2)}) copy-start(bf16[128,544]{1,0:T(8,128)(2,1)} %get-tuple-element.667) | copy-start | bytes 417796 | tf_op jit(solution)/shard_map/while
  276.6 48.1 %copy-start.1 = (bf16[1536,1024]{1,0:T(8,128)(2,1)S(1)}, bf16[1536,1024]{1,0:T(8,128)(2,1)}, u32[]{:S(2)}) copy-start(bf16[1536,1024]{1,0:T(8,128)(2,1)} %get-tuple-element.1109) | copy-start | bytes 9437188
  351.7 12.6 %copy-start.15 = (bf16[128,576]{1,0:T(8,128)(2,1)S(1)}, bf16[128,576]{1,0:T(8,128)(2,1)}, u32[]{:S(2)}) copy-start(bf16[128,576]{1,0:T(8,128)(2,1)} %get-tuple-element.737) | copy-start | bytes 442372 | tf_op jit(solution)/shard_map/while
  351.7 12.6 %copy-start.17 = (bf16[128,544]{1,0:T(8,128)(2,1)S(1)}, bf16[128,544]{1,0:T(8,128)(2,1)}, u32[]{:S(2)}) copy-start(bf16[128,544]{1,0:T(8,128)(2,1)} %get-tuple-element.736) | copy-start | bytes 417796 | tf_op jit(solution)/shard_map/while
  397.6 12.6 %copy-start.15 = (bf16[128,576]{1,0:T(8,128)(2,1)S(1)}, bf16[128,576]{1,0:T(8,128)(2,1)}, u32[]{:S(2)}) copy-start(bf16[128,576]{1,0:T(8,128)(2,1)} %get-tuple-element.737) | copy-start | bytes 442372 | tf_op jit(solution)/shard_map/while
  397.6 12.6 %copy-start.17 = (bf16[128,544]{1,0:T(8,128)(2,1)S(1)}, bf16[128,544]{1,0:T(8,128)(2,1)}, u32[]{:S(2)}) copy-start(bf16[128,544]{1,0:T(8,128)(2,1)} %get-tuple-element.736) | copy-start | bytes 417796 | tf_op jit(solution)/shard_map/while
  443.4 12.6 %copy-start.15 = (bf16[128,576]{1,0:T(8,128)(2,1)S(1)}, bf16[128,576]{1,0:T(8,128)(2,1)}, u32[]{:S(2)}) copy-start(bf16[128,576]{1,0:T(8,128)(2,1)} %get-tuple-element.737) | copy-start | bytes 442372 | tf_op jit(solution)/shard_map/while
  443.4 12.6 %copy-start.17 = (bf16[128,544]{1,0:T(8,128)(2,1)S(1)}, bf16[128,544]{1,0:T(8,128)(2,1)}, u32[]{:S(2)}) copy-start(bf16[128,544]{1,0:T(8,128)(2,1)} %get-tuple-element.736) | copy-start | bytes 417796 | tf_op jit(solution)/shard_map/while
  489.2 12.6 %copy-start.15 = (bf16[128,576]{1,0:T(8,128)(2,1)S(1)}, bf16[128,576]{1,0:T(8,128)(2,1)}, u32[]{:S(2)}) copy-start(bf16[128,576]{1,0:T(8,128)(2,1)} %get-tuple-element.737) | copy-start | bytes 442372 | tf_op jit(solution)/shard_map/while
  489.2 12.6 %copy-start.17 = (bf16[128,544]{1,0:T(8,128)(2,1)S(1)}, bf16[128,544]{1,0:T(8,128)(2,1)}, u32[]{:S(2)}) copy-start(bf16[128,544]{1,0:T(8,128)(2,1)} %get-tuple-element.736) | copy-start | bytes 417796 | tf_op jit(solution)/shard_map/while
  (59 other events, 526.4 us)
Sparse Core Ops, SparseCore 0:
  39.3 14.3 all-gather.2
  259.4 10.2 all-gather.4
where the time goes:
time: 520 us; the launch traced here: 518 us
  local copies, waits for them, and re-layouts  381 us (73%)
  blocking collectives  34.8 us (7%)
  matrix products  23.9 us (5%)
  waiting for transfers between devices  22.9 us (4%)
  other arithmetic  21.4 us (4%)
  between operations  14.2 us (3%)
  loops' own time  13.2 us (3%)
  starting transfers between devices  6.27 us (1%)
    while x416, local copies, waits for them, and re-layouts  178 us
    slice x120, local copies, waits for them, and re-layouts, shift_slots(): segment[:, :segment.shape[1] - moved * BLK]  98.7 us
    dynamic_slice x136, local copies, waits for them, and re-layouts, one_group(): lax.dynamic_slice_in_dim(segment, first_slot * BLK, column_slots * BLK, 1)  45.4 us
    psum x1, blocking collectives, per_device(): total_squared = lax.psum(trace_squared, ('row', 'col'))  34.8 us
    dot_general x8, matrix products, one_group(): jnp.einsum('gak,gkn->gan', left_rows, gathered, preferred_element_type=jn...  23.9 us
    ppermute x1, waiting for transfers between devices, extended_2(): before = lax.ppermute(last, axis, up)  21.1 us
    another operation x2, loops' own time, band_part(): lax.map(one_group, jnp.arange(block_rows // group_rows, dtype=jnp.int32))  13.2 us
    transpose x2, other arithmetic, diagonal_sum(): jnp.diagonal(values.reshape(block_rows, BLK, slot_total, BLK), axis1=1, a...  11.4 us
  transfers between devices with their start and end apart: 4, of which 2 were waited for; matrix products, arithmetic and copies ran while one was open for 8% of the time, Pallas kernels for 0%

commit v1 on v0

--- a/solution.py
+++ b/solution.py
@@ -140,7 +140,7 @@
         collect_half,
     )
     trace_squared = diagonal_sum(squared, chosen)
-    total_squared = lax.psum(trace_squared, ("row", "col"))
+    total_squared = lax.psum(lax.psum(trace_squared, "col"), "row")
     order_total = block_total * BLK
     traces = jnp.stack([total_kept, total_squared]) / order_total
     return (purified, traces)

time: 520 us -> 546 us (1.050)
  blocking collectives: 34.8 us -> 55.8 us
    psum x1 -> x3, blocking collectives: 34.8 us -> 55.8 us  [the longest x1 30.3 us: per_device(): total_kept = lax.psum(trace_kept, ('row', 'col'))]
where the time goes in v1:
time: 546 us; the launch traced here: 544 us
  local copies, waits for them, and re-layouts  386 us (71%)
  blocking collectives  55.8 us (10%)
  matrix products  23.9 us (4%)
  waiting for transfers between devices  22.9 us (4%)
  other arithmetic  21.3 us (4%)
  between operations  14.2 us (3%)
  loops' own time  13.2 us (2%)
  starting transfers between devices  6.27 us (1%)
    while x416, local copies, waits for them, and re-layouts  182 us
    slice x120, local copies, waits for them, and re-layouts, shift_slots(): segment[:, :segment.shape[1] - moved * BLK]  99.2 us
    dynamic_slice x136, local copies, waits for them, and re-layouts, one_group(): lax.dynamic_slice_in_dim(segment, first_slot * BLK, column_slots * BLK, 1)  45.5 us
    psum x1, blocking collectives, per_device(): total_kept = lax.psum(trace_kept, ('row', 'col'))  30.3 us
    psum x2, blocking collectives, per_device(): total_squared = lax.psum(lax.psum(trace_squared, 'col'), 'row')  25.4 us
    dot_general x8, matrix products, one_group(): jnp.einsum('gak,gkn->gan', left_rows, gathered, preferred_element_type=jn...  23.9 us
    ppermute x1, waiting for transfers between devices, extended_2(): before = lax.ppermute(last, axis, up)  21.1 us
    another operation x2, loops' own time, band_part(): lax.map(one_group, jnp.arange(block_rows // group_rows, dtype=jnp.int32))  13.2 us
  transfers between devices with their start and end apart: 4, of which 2 were waited for; matrix products, arithmetic and copies ran while one was open for 8% of the time, Pallas kernels for 0%

profile of v1, /device:TPU:0, one launch (start us, length us, event | category | flops | bytes accessed | tf_op | source)
XLA Modules:
  0.0 543.8 jit_solution(13312325032449988135)
XLA Ops:
  8.4 2.1 mul.804
  10.6 4.9 collective-permute-start
  16.8 21.1 %collective-permute-done = bf16[512,512]{1,0:T(8,128)(2,1)S(1)} collective-permute-done((bf16[512,512]{1,0:T(8,128)(2,1)S(1)}, bf16[512,512]{1,0:T(8,128)(2,1)S(1)}, u32[]{:S(2)}, u32[]{:S(2)}) %collective-permute-start) | collective-permute-done | bytes 524320 | tf_op jit(solution)/shard_map/ppermute | solution.py:16
  40.5 4.3 copy.7
  44.8 2.4 mul.808.clone
  47.1 4.7 mul.809
  51.8 1.8 all-gather.3.cloned.1.call-done
  53.7 2.3 slice.442
  57.1 203.0 %while.26 = (s32[]{:T(128)}, f32[4,128,512]{2,1,0:T(8,128)}, s32[4]{0:T(128)S(1)}, bf16[512,1024]{1,0:T(8,128)(2,1)}, bf16[1536,1024]{1,0:T(8,128)(2,1)}, /*inde...) while((s32[]{:T(128)}, f32[4,128,512]{2,1,0:T(8,128)}, ...), condition=%wide.region_1.2_spmd, body=%wide.region_0.1_spmd.sunk | while | flops 134217904 | bytes 56200764 | solution.py:83
  58.7 1.7 constant_dynamic-slice_fusion.65
  104.1 3.0 fusion.27
  109.5 1.7 constant_dynamic-slice_fusion.65
  154.8 3.0 fusion.27
  205.6 3.0 fusion.27
  256.3 3.0 fusion.27
  260.1 2.5 fusion.4
  262.6 4.6 multiply_bitcast_fusion
  267.2 2.8 gather_fusion
  270.0 2.7 reshape_reshape.10
  272.7 7.3 %copy.8 = f32[16,32,16,32]{2,0,3,1:T(8,128)} copy(f32[16,32,16,32]{3,2,1,0:T(8,128)} %reshape_reshape.10) | data formatting | bytes 2097152 | tf_op jit(solution)/shard_map/reshape;reshape | solution.py:32
  280.0 6.8 %fusion = bf16[16,16,32,32]{1,0,3,2:T(8,128)(2,1)} fusion(f32[16,32,16,32]{2,0,3,1:T(8,128)} %copy.8, f32[16,16]{1,0:T(8,128)S(1)} %get-tuple-element.401), kind=kLoop, calls=%fused_computation.163 | loop fusion | flops 524288 | bytes 1573888 | tf_op jit(solution)/shard_map/jit(diagonal)/transpose | solution.py:90
  286.8 2.8 gather_fusion.1
  290.3 3.2 psum.22
  293.5 22.3 %psum.23 = f32[1]{0:T(128)} all-reduce(f32[1]{0:T(128)} %bitcast.140), channel_id=1, replica_groups=mesh['snap'=2,'row'=8,'col'=2] {'row'}, use_global_device_ids=true, to_apply=%region_8.9 | all-reduce | flops 1 | bytes 8 | tf_op jit(solution)/shard_map/psum | solution.py:143
  315.7 30.3 %psum.21 = f32[1]{0:T(128)} all-reduce(f32[1]{0:T(128)} %bitcast.138), channel_id=1, replica_groups=mesh['snap'=2,'row'=8,'col'=2] {'row','col'}, use_global_device_ids=true, to_apply=%region_5.6 | all-reduce | flops 1 | bytes 8 | tf_op jit(solution)/shard_map/psum | solution.py:123
  346.1 1.8 maximum_multiply_fusion
  349.0 185.2 %while.27 = (s32[]{:T(128)}, f32[4,128,512]{2,1,0:T(8,128)}, s32[4]{0:T(128)S(1)}, bf16[512,1024]{1,0:T(8,128)(2,1)}, bf16[1536,1024]{1,0:T(8,128)(2,1)S(1)}, /*...) while((s32[]{:T(128)}, f32[4,128,512]{2,1,0:T(8,128)}, ...), condition=%wide.region_3.4_spmd, body=%wide.region_2.3_spmd.sunk | while | flops 134217904 | bytes 43617860 | solution.py:83
  391.6 3.0 fusion.31
  437.9 3.0 fusion.31
  484.2 3.0 fusion.31
  530.5 3.0 fusion.31
  534.2 2.8 fusion.3
  (728 shorter events, 355.7 us)
Async XLA Ops:
  7.2 46.5 %all-gather.3.cloned.1.call-start = ((), (), s32[]{:S(2)}) async-start(), calls=%async_computation | async-start | bytes 4718592 | tf_op jit(solution)/shard_map/all_gather | solution.py:126
  10.6 27.3 %collective-permute-start = (bf16[512,512]{1,0:T(8,128)(2,1)S(1)}, bf16[512,512]{1,0:T(8,128)(2,1)S(1)}, u32[]{:S(2)}, u32[]{:S(2)}) collective-permute-start(bf16[512,512]{1,0:T(8,128)(2,1)S(1)} %mul.805), channel_id=1, source_target_pairs={{0,2},{2,4},{4,6},{6,8},{8,10},{10,12},{12,14},{1,3},{3,5},{5,7},{... | collective-permute-start | bytes 1572872 | tf_op jit(solution)/shard_map/ppermute | solution.py:16
  15.5 22.4 %collective-permute-start.1 = (bf16[512,512]{1,0:T(8,128)(2,1)S(1)}, bf16[512,512]{1,0:T(8,128)(2,1)S(1)}, u32[]{:S(2)}, u32[]{:S(2)}) collective-permute-start(bf16[512,512]{1,0:T(8,128)(2,1)S(1)} %mul.805), channel_id=1, source_target_pairs={{2,0},{4,2},{6,4},{8,6},{10,8},{12,10},{14,12},{3,1},{5,3},{7,5},{... | collective-permute-start | bytes 1572872 | tf_op jit(solution)/shard_map/ppermute | solution.py:17
  39.2 308.7 %all-gather.5.cloned.1.call-start = ((), (), s32[]{:S(2)}) async-start(), calls=%async_computation.1 | async-start | bytes 1572864 | tf_op jit(solution)/shard_map/all_gather | solution.py:130
  57.1 13.3 %copy-start = (bf16[1536,1024]{1,0:T(8,128)(2,1)S(1)}, bf16[1536,1024]{1,0:T(8,128)(2,1)}, u32[]{:S(2)}) copy-start(bf16[1536,1024]{1,0:T(8,128)(2,1)} %get-tuple-element.864) | copy-start | bytes 9437188 | tf_op jit(solution)/shard_map/while
  88.3 11.8 %copy-start.18 = (bf16[128,640]{1,0:T(8,128)(2,1)S(1)}, bf16[128,640]{1,0:T(8,128)(2,1)}, u32[]{:S(2)}) copy-start(bf16[128,640]{1,0:T(8,128)(2,1)} %get-tuple-element.662) | copy-start | bytes 491524 | tf_op jit(solution)/shard_map/while
  88.3 11.8 %copy-start.20 = (bf16[128,608]{1,0:T(8,128)(2,1)S(1)}, bf16[128,608]{1,0:T(8,128)(2,1)}, u32[]{:S(2)}) copy-start(bf16[128,608]{1,0:T(8,128)(2,1)} %get-tuple-element.661) | copy-start | bytes 466948 | tf_op jit(solution)/shard_map/while
  88.6 12.9 %copy-start.14 = (bf16[128,576]{1,0:T(8,128)(2,1)S(1)}, bf16[128,576]{1,0:T(8,128)(2,1)}, u32[]{:S(2)}) copy-start(bf16[128,576]{1,0:T(8,128)(2,1)} %get-tuple-element.666) | copy-start | bytes 442372 | tf_op jit(solution)/shard_map/while
  88.7 12.9 %copy-start.16 = (bf16[128,544]{1,0:T(8,128)(2,1)S(1)}, bf16[128,544]{1,0:T(8,128)(2,1)}, u32[]{:S(2)}) copy-start(bf16[128,544]{1,0:T(8,128)(2,1)} %get-tuple-element.665) | copy-start | bytes 417796 | tf_op jit(solution)/shard_map/while
  107.8 13.3 %copy-start = (bf16[1536,1024]{1,0:T(8,128)(2,1)S(1)}, bf16[1536,1024]{1,0:T(8,128)(2,1)}, u32[]{:S(2)}) copy-start(bf16[1536,1024]{1,0:T(8,128)(2,1)} %get-tuple-element.864) | copy-start | bytes 9437188 | tf_op jit(solution)/shard_map/while
  139.1 11.8 %copy-start.18 = (bf16[128,640]{1,0:T(8,128)(2,1)S(1)}, bf16[128,640]{1,0:T(8,128)(2,1)}, u32[]{:S(2)}) copy-start(bf16[128,640]{1,0:T(8,128)(2,1)} %get-tuple-element.662) | copy-start | bytes 491524 | tf_op jit(solution)/shard_map/while
  139.1 11.8 %copy-start.20 = (bf16[128,608]{1,0:T(8,128)(2,1)S(1)}, bf16[128,608]{1,0:T(8,128)(2,1)}, u32[]{:S(2)}) copy-start(bf16[128,608]{1,0:T(8,128)(2,1)} %get-tuple-element.661) | copy-start | bytes 466948 | tf_op jit(solution)/shard_map/while
  139.4 12.9 %copy-start.14 = (bf16[128,576]{1,0:T(8,128)(2,1)S(1)}, bf16[128,576]{1,0:T(8,128)(2,1)}, u32[]{:S(2)}) copy-start(bf16[128,576]{1,0:T(8,128)(2,1)} %get-tuple-element.666) | copy-start | bytes 442372 | tf_op jit(solution)/shard_map/while
  139.4 12.9 %copy-start.16 = (bf16[128,544]{1,0:T(8,128)(2,1)S(1)}, bf16[128,544]{1,0:T(8,128)(2,1)}, u32[]{:S(2)}) copy-start(bf16[128,544]{1,0:T(8,128)(2,1)} %get-tuple-element.665) | copy-start | bytes 417796 | tf_op jit(solution)/shard_map/while
  158.6 13.3 %copy-start = (bf16[1536,1024]{1,0:T(8,128)(2,1)S(1)}, bf16[1536,1024]{1,0:T(8,128)(2,1)}, u32[]{:S(2)}) copy-start(bf16[1536,1024]{1,0:T(8,128)(2,1)} %get-tuple-element.864) | copy-start | bytes 9437188 | tf_op jit(solution)/shard_map/while
  189.8 11.8 %copy-start.18 = (bf16[128,640]{1,0:T(8,128)(2,1)S(1)}, bf16[128,640]{1,0:T(8,128)(2,1)}, u32[]{:S(2)}) copy-start(bf16[128,640]{1,0:T(8,128)(2,1)} %get-tuple-element.662) | copy-start | bytes 491524 | tf_op jit(solution)/shard_map/while
  189.8 11.8 %copy-start.20 = (bf16[128,608]{1,0:T(8,128)(2,1)S(1)}, bf16[128,608]{1,0:T(8,128)(2,1)}, u32[]{:S(2)}) copy-start(bf16[128,608]{1,0:T(8,128)(2,1)} %get-tuple-element.661) | copy-start | bytes 466948 | tf_op jit(solution)/shard_map/while
  190.1 12.9 %copy-start.14 = (bf16[128,576]{1,0:T(8,128)(2,1)S(1)}, bf16[128,576]{1,0:T(8,128)(2,1)}, u32[]{:S(2)}) copy-start(bf16[128,576]{1,0:T(8,128)(2,1)} %get-tuple-element.666) | copy-start | bytes 442372 | tf_op jit(solution)/shard_map/while
  190.2 12.9 %copy-start.16 = (bf16[128,544]{1,0:T(8,128)(2,1)S(1)}, bf16[128,544]{1,0:T(8,128)(2,1)}, u32[]{:S(2)}) copy-start(bf16[128,544]{1,0:T(8,128)(2,1)} %get-tuple-element.665) | copy-start | bytes 417796 | tf_op jit(solution)/shard_map/while
  209.3 13.3 %copy-start = (bf16[1536,1024]{1,0:T(8,128)(2,1)S(1)}, bf16[1536,1024]{1,0:T(8,128)(2,1)}, u32[]{:S(2)}) copy-start(bf16[1536,1024]{1,0:T(8,128)(2,1)} %get-tuple-element.864) | copy-start | bytes 9437188 | tf_op jit(solution)/shard_map/while
  240.6 11.8 %copy-start.18 = (bf16[128,640]{1,0:T(8,128)(2,1)S(1)}, bf16[128,640]{1,0:T(8,128)(2,1)}, u32[]{:S(2)}) copy-start(bf16[128,640]{1,0:T(8,128)(2,1)} %get-tuple-element.662) | copy-start | bytes 491524 | tf_op jit(solution)/shard_map/while
  240.9 12.9 %copy-start.14 = (bf16[128,576]{1,0:T(8,128)(2,1)S(1)}, bf16[128,576]{1,0:T(8,128)(2,1)}, u32[]{:S(2)}) copy-start(bf16[128,576]{1,0:T(8,128)(2,1)} %get-tuple-element.666) | copy-start | bytes 442372 | tf_op jit(solution)/shard_map/while
  240.9 12.9 %copy-start.16 = (bf16[128,544]{1,0:T(8,128)(2,1)S(1)}, bf16[128,544]{1,0:T(8,128)(2,1)}, u32[]{:S(2)}) copy-start(bf16[128,544]{1,0:T(8,128)(2,1)} %get-tuple-element.665) | copy-start | bytes 417796 | tf_op jit(solution)/shard_map/while
  280.0 69.0 %copy-start.1 = (bf16[1536,1024]{1,0:T(8,128)(2,1)S(1)}, bf16[1536,1024]{1,0:T(8,128)(2,1)}, u32[]{:S(2)}) copy-start(bf16[1536,1024]{1,0:T(8,128)(2,1)} %get-tuple-element.1107) | copy-start | bytes 9437188
  376.2 12.9 %copy-start.15 = (bf16[128,576]{1,0:T(8,128)(2,1)S(1)}, bf16[128,576]{1,0:T(8,128)(2,1)}, u32[]{:S(2)}) copy-start(bf16[128,576]{1,0:T(8,128)(2,1)} %get-tuple-element.735) | copy-start | bytes 442372 | tf_op jit(solution)/shard_map/while
  376.2 12.9 %copy-start.17 = (bf16[128,544]{1,0:T(8,128)(2,1)S(1)}, bf16[128,544]{1,0:T(8,128)(2,1)}, u32[]{:S(2)}) copy-start(bf16[128,544]{1,0:T(8,128)(2,1)} %get-tuple-element.734) | copy-start | bytes 417796 | tf_op jit(solution)/shard_map/while
  422.5 12.9 %copy-start.15 = (bf16[128,576]{1,0:T(8,128)(2,1)S(1)}, bf16[128,576]{1,0:T(8,128)(2,1)}, u32[]{:S(2)}) copy-start(bf16[128,576]{1,0:T(8,128)(2,1)} %get-tuple-element.735) | copy-start | bytes 442372 | tf_op jit(solution)/shard_map/while
  422.5 12.9 %copy-start.17 = (bf16[128,544]{1,0:T(8,128)(2,1)S(1)}, bf16[128,544]{1,0:T(8,128)(2,1)}, u32[]{:S(2)}) copy-start(bf16[128,544]{1,0:T(8,128)(2,1)} %get-tuple-element.734) | copy-start | bytes 417796 | tf_op jit(solution)/shard_map/while
  468.8 12.9 %copy-start.15 = (bf16[128,576]{1,0:T(8,128)(2,1)S(1)}, bf16[128,576]{1,0:T(8,128)(2,1)}, u32[]{:S(2)}) copy-start(bf16[128,576]{1,0:T(8,128)(2,1)} %get-tuple-element.735) | copy-start | bytes 442372 | tf_op jit(solution)/shard_map/while
  468.8 12.9 %copy-start.17 = (bf16[128,544]{1,0:T(8,128)(2,1)S(1)}, bf16[128,544]{1,0:T(8,128)(2,1)}, u32[]{:S(2)}) copy-start(bf16[128,544]{1,0:T(8,128)(2,1)} %get-tuple-element.734) | copy-start | bytes 417796 | tf_op jit(solution)/shard_map/while
  515.1 12.9 %copy-start.15 = (bf16[128,576]{1,0:T(8,128)(2,1)S(1)}, bf16[128,576]{1,0:T(8,128)(2,1)}, u32[]{:S(2)}) copy-start(bf16[128,576]{1,0:T(8,128)(2,1)} %get-tuple-element.735) | copy-start | bytes 442372 | tf_op jit(solution)/shard_map/while
  515.1 12.9 %copy-start.17 = (bf16[128,544]{1,0:T(8,128)(2,1)S(1)}, bf16[128,544]{1,0:T(8,128)(2,1)}, u32[]{:S(2)}) copy-start(bf16[128,544]{1,0:T(8,128)(2,1)} %get-tuple-element.734) | copy-start | bytes 417796 | tf_op jit(solution)/shard_map/while
  (59 other events, 534.8 us)
Sparse Core Ops, SparseCore 0:
  39.3 14.3 all-gather.2
  262.7 10.2 all-gather.4
